TPU v7x, 32 devices: a whole 2x2x4 slice. The times are simulated.
32 devices in a mesh: gx: 4 (over y, x), gy: 2 (over core), gz: 4 (over z).
Axes of the slice: x: 2, y: 2, z: 4, core: 2. Of those that a mesh axis runs over, the one named last changes fastest.
Arguments:
- volume: float32 [512, 128, 512], P('gx', 'gy', 'gz'), may hold values from -6 to 6
Outputs:
- prefix: float32 [512, 128, 512], P('gx', 'gy', 'gz')
- box_sum: float32 [512, 128, 512], P('gx', 'gy', 'gz')
All inputs are finite; a program needn't handle non-finite values.
Results may differ from a plain program's by a relative error of at most 0.00055.
Values sent between devices are 32-bit elements; how exact they have to be, the bound alone decides.
A program may use at most 128 MiB of HBM per device.

v0:
```python
import functools
import math

import jax
import jax.numpy as jnp
from jax import lax
from jax.experimental import pallas as pl
from jax.experimental.pallas import tpu as pltpu
from jax.sharding import PartitionSpec as P

F32 = jnp.float32
BF16 = jnp.bfloat16
MESH = pl.DeviceIdType.MESH
USED = (0, 2, 3, 4, 5)
PLANES = 16


def split(a, axis):
    hi = a.astype(BF16)
    lo = (a - hi.astype(F32)).astype(BF16)
    return jnp.concatenate([hi, lo], axis=axis)


def source_index(kind, length):
    return {2: length - 2, 3: length - 1, 4: 0, 5: 1}[kind]


def selector(length):
    kind = lax.broadcasted_iota(jnp.int32, (8, length), 0)
    at = lax.broadcasted_iota(jnp.int32, (8, length), 1)
    pick = kind == 0
    for k in (2, 3, 4, 5):
        pick = pick | ((kind == k) & (at == source_index(k, length)))
    one = jnp.where(pick, 1.0, 0.0).astype(BF16)
    return jnp.concatenate([one, one], axis=1)


def z_sources(rows):
    return lax.dot_general(
        selector(rows.shape[1]),
        split(rows, 1),
        (((1,), (1,)), ((), ())),
        preferred_element_type=F32,
    )


def sources_kernel(ny, nz, v_ref, x_ref, y_ref, z_ref, zy_ref, zx_ref, zxy_ref):
    i, steps = pl.program_id(0), pl.num_programs(0)
    nx = steps * PLANES
    blocks = PLANES * ny // 128
    zrows = z_ref.shape[0] // 8

    @pl.when(i == 0)
    def _():
        x_ref[...] = jnp.zeros_like(x_ref)
        y_ref[...] = jnp.zeros_like(y_ref)
        x_ref[4] = v_ref[pl.ds(0, ny), :]
        x_ref[5] = v_ref[pl.ds(ny, ny), :]

    total = v_ref[pl.ds(0, ny), :]
    for x in range(1, PLANES):
        total = total + v_ref[pl.ds(x * ny, ny), :]
    x_ref[0] = x_ref[0] + total
    at = pl.ds(pl.multiple_of(i * PLANES, PLANES), PLANES)
    y_ref[0, at, :] = jnp.sum(v_ref[...].reshape(PLANES, ny, nz), axis=1)
    for k in (2, 3, 4, 5):
        y_ref[k, at, :] = v_ref[pl.ds(source_index(k, ny), PLANES, stride=ny), :]
    found = z_sources(v_ref[...])
    for b in range(blocks):
        z_ref[pl.ds(i * blocks + b, 8, stride=zrows), :] = found[:, b * 128 : (b + 1) * 128]

    @pl.when(i == steps - 1)
    def _():
        x_ref[2] = v_ref[pl.ds((PLANES - 2) * ny, ny), :]
        x_ref[3] = v_ref[pl.ds((PLANES - 1) * ny, ny), :]
        count = y_ref.shape[1] - 8
        planes = x_ref[...]
        y_ref[0, pl.ds(count, 8), :] = jnp.sum(planes, axis=1)
        for k in (2, 3, 4, 5):
            y_ref[k, pl.ds(count, 8), :] = planes[:, source_index(k, ny), :]
        for k in range(8):
            zy_ref[k] = z_sources(y_ref[k, pl.ds(0, count), :])
        pairs = planes.reshape(4, 2 * ny, nz)
        for k in range(4):
            zx_ref[k] = z_sources(pairs[k])
        corner = y_ref[:, pl.ds(count, 8), :].reshape(64, nz)
        zxy_ref[0] = z_sources(jnp.concatenate([corner, jnp.zeros_like(corner)], axis=0))


class Exchange:
    def __init__(self, send, recv):
        self.send, self.recv, self.count = send, recv, 0

    def start(self, axis, shift, src, dst):
        n, me = lax.axis_size(axis), lax.axis_index(axis)
        at = self.count
        self.count += 1
        copy = pltpu.make_async_remote_copy(
            src_ref=src,
            dst_ref=dst,
            send_sem=self.send.at[at],
            recv_sem=self.recv.at[at],
            device_id={axis: lax.rem(me + shift + n, n)},
            device_id_type=MESH,
        )
        sends = (me + shift >= 0) & (me + shift < n)
        receives = (me - shift >= 0) & (me - shift < n)
        pl.when(sends)(copy.start)
        return sends, receives, copy

    def layers(self, axis, src, carry, halo):
        out = []
        n = lax.axis_size(axis)
        if n > 1:
            out.append(self.start(axis, 1, src.at[pl.ds(2, 2)], halo.at[pl.ds(0, 2)]))
            out.append(self.start(axis, -1, src.at[pl.ds(4, 2)], halo.at[pl.ds(2, 2)]))
        for d in range(1, n):
            out.append(self.start(axis, d, src.at[pl.ds(0, 1)], carry.at[pl.ds(d - 1, 1)]))
        return out

    def whole(self, axis, src, slots):
        n = lax.axis_size(axis)
        out = [self.start(axis, d, src, slots.at[d - 1]) for d in range(1, n)]
        if n > 1:
            out.append(self.start(axis, -1, src, slots.at[n - 1]))
        return out


def arrived(copies):
    for _, receives, copy in copies:
        pl.when(receives)(copy.wait_recv)


def sent(copies):
    for sends, _, copy in copies:
        pl.when(sends)(copy.wait_send)


def carry_total(carry, n):
    total = carry[0]
    for d in range(1, n - 1):
        total = total + carry[d]
    return total


def put_layers(out_ref, carry, halo, n):
    out_ref[0] = carry_total(carry, n)
    out_ref[1] = jnp.zeros_like(out_ref[1])
    for k in range(4):
        out_ref[2 + k] = halo[k]
    for k in (6, 7):
        out_ref[k] = jnp.zeros_like(out_ref[k])


def combined(slots, n, kind):
    total = slots[0]
    for d in range(1, n - 1):
        total = total + slots[d]
    zero = jnp.zeros_like(total)
    result = jnp.where(kind == 0, total, zero)
    result = jnp.where((kind == 2) | (kind == 3), slots[0], result)
    return jnp.where((kind == 4) | (kind == 5), slots[n - 1], result)


def exchange_kernel(
    x_in, y_in, z_in, zy_in, zx_in, zxy_in,
    x_out, y_out, z_out, zy_out, zx_out, zxy_out,
    xc, xh, yc, yh, zc, zh, zyc, zyh, zyk, zxc, zxh, corner_y, corner_x_src, corner_x,
    z1_src, z1, z2_src, z2, send, recv,
):
    sizes = {a: lax.axis_size(a) for a in ("gx", "gy", "gz")}
    nx, ny, nz = sizes["gx"], sizes["gy"], sizes["gz"]
    for ref in (xc, xh, yc, yh, zc, zh, zyc, zyh, zxc, zxh, corner_y, corner_x, z1, z2):
        ref[...] = jnp.zeros_like(ref)
    barrier = pltpu.get_barrier_semaphore()
    for axis, n in sizes.items():
        me = lax.axis_index(axis)
        for d in range(1, n):
            pl.semaphore_signal(
                barrier, inc=1, device_id={axis: lax.rem(me + d, n)}, device_id_type=MESH
            )
    pl.semaphore_wait(barrier, nx + ny + nz - 3)

    ex = Exchange(send, recv)
    to_y = ex.layers("gy", y_in, yc, yh)
    to_y += ex.layers("gy", zy_in, zyc, zyh)
    to_y += ex.whole("gy", zxy_in, corner_y)
    to_x = ex.layers("gx", x_in, xc, xh)
    to_x.append(ex.start("gx", 1, zx_in.at[pl.ds(1, 1)], zxh.at[pl.ds(0, 1)]))
    to_x.append(ex.start("gx", -1, zx_in.at[pl.ds(2, 1)], zxh.at[pl.ds(1, 1)]))
    for d in range(1, nx):
        to_x.append(ex.start("gx", d, zx_in.at[pl.ds(0, 1)], zxc.at[pl.ds(d - 1, 1)]))
    to_z = ex.layers("gz", z_in, zc, zh)

    lane = lax.broadcasted_iota(jnp.int32, (1, 8, 128), 2)
    row = lax.broadcasted_iota(jnp.int32, (1, 8, 128), 1)
    arrived(to_y)
    count = y_in.shape[1] - 8
    put_layers(y_out, yc, yh, ny)
    put_layers(zyk, zyc, zyh, ny)
    z1_src[...] = zyk[...]
    more_z = ex.whole("gz", z1_src, z1)
    corner_x_src[pl.ds(0, 8)] = y_out[:, pl.ds(count, 8), :]
    corner_x_src[pl.ds(8, 1)] = combined(corner_y, ny, lane // 8)
    more_x = ex.whole("gx", corner_x_src, corner_x)

    arrived(to_x)
    put_layers(x_out, xc, xh, nx)
    z2_src[pl.ds(0, 1)] = carry_total(zxc, nx)[None]
    z2_src[pl.ds(1, 2)] = zxh[...]
    z2_src[pl.ds(3, 1)] = jnp.zeros((1, 8, 128), F32)
    arrived(more_x)
    got = corner_x.at[:, pl.ds(0, 8)]
    y_out[:, pl.ds(count, 8), :] = combined(got, nx, row)
    z2_src[pl.ds(4, 1)] = combined(corner_x.at[:, pl.ds(8, 1)], nx, lax.rem(lane, 8))
    last_z = ex.whole("gz", z2_src, z2)

    arrived(to_z)
    put_layers(z_out, zc, zh, nz)
    arrived(more_z)
    zy_out[...] = combined(z1, nz, row)
    arrived(last_z)
    zx_out[...] = combined(z2.at[:, pl.ds(0, 4)], nz, row)
    zxy_out[...] = combined(z2.at[:, pl.ds(4, 1)], nz, row)
    sent(to_y + to_x + to_z + more_z + more_x + last_z)


def z_weights(nz):
    rows = lax.broadcasted_iota(jnp.int32, (nz, nz), 0)
    cols = lax.broadcasted_iota(jnp.int32, (nz, nz), 1)
    lower = jnp.where(rows <= cols, 1.0, 0.0).astype(BF16)
    band = jnp.where(jnp.abs(rows - cols) <= 2, 1.0, 0.0).astype(BF16)
    half = jnp.concatenate([lower, band], axis=1)
    kind = lax.broadcasted_iota(jnp.int32, (8, nz), 0)
    at = lax.broadcasted_iota(jnp.int32, (8, nz), 1)
    add = (kind == 2) & (at == 0)
    add |= (kind == 3) & (at <= 1)
    add |= (kind == 4) & (at >= nz - 2)
    add |= (kind == 5) & (at == nz - 1)
    edge = jnp.concatenate(
        [jnp.where(kind == 0, 1.0, 0.0).astype(BF16), jnp.where(add, 1.0, 0.0).astype(BF16)], axis=1
    )
    return jnp.concatenate([half, half], axis=0), jnp.concatenate([edge, edge], axis=0)


def along_z(rows, edges, w_ref, e_ref):
    main = jnp.dot(split(rows, 1), w_ref[...], preferred_element_type=F32)
    return main + lax.dot_general(
        split(edges, 0), e_ref[...], (((0,), (0,)), ((), ())), preferred_element_type=F32
    )


def final_kernel(
    ny, nz, scale,
    v_ref, x_ref, y_ref, z_ref, zy_ref, zx_ref, zxy_ref, w_ref, e_ref,
    prefix_ref, box_ref,
    grid_z, rows_y, plane_z, run, tall, boxed,
):
    i, steps = pl.program_id(0), pl.num_programs(0)
    count = y_ref.shape[1] - 8
    blocks = PLANES * ny // 128
    zrows = z_ref.shape[0] // 8

    def y_prefix(piece, start):
        row = lax.broadcasted_iota(jnp.int32, (1, 8, nz), 1)
        c = piece.reshape(ny // 8, 8, nz)
        for step in (1, 2, 4):
            c = c + jnp.where(row >= step, pltpu.roll(c, step, 1), 0.0)
        out = []
        for k in range(ny // 8):
            out.append(c[k] + start)
            start = out[-1][7:8]
        return jnp.concatenate(out, axis=0)

    def y_box(slot, piece, before, after):
        tall[slot, pl.ds(8, ny), :] = piece
        tall[slot, pl.ds(6, 1), :] = before[0]
        tall[slot, pl.ds(7, 1), :] = before[1]
        tall[slot, pl.ds(8 + ny, 1), :] = after[0]
        tall[slot, pl.ds(9 + ny, 1), :] = after[1]
        total = piece
        for d in (6, 7, 9, 10):
            total = total + tall[slot, pl.ds(d, ny), :]
        return total

    def row_of(k, x, part):
        return rows_y[k, pl.ds(x, 1), pl.ds(part * nz, nz)]

    @pl.when(i == 0)
    def _():
        for k in USED:
            rows_y[k, pl.ds(0, count), :] = along_z(
                y_ref[k, pl.ds(0, count), :], zy_ref[k], w_ref, e_ref
            )
        corner = along_z(
            y_ref[:, pl.ds(count, 8), :].reshape(64, nz), zxy_ref[0][:, :64], w_ref, e_ref
        )
        rows_y[:, pl.ds(count, 8), :] = corner.reshape(8, 8, 2 * nz)
        edges = jnp.concatenate([zx_ref[k] for k in range(4)], axis=1)
        plane_z[...] = along_z(x_ref[...].reshape(8 * ny, nz), edges, w_ref, e_ref)
        run[...] = y_prefix(plane_z[pl.ds(0, ny), pl.ds(0, nz)], row_of(0, count, 0))
        for k, to in ((2, 0), (3, 1), (4, count + 2), (5, count + 3)):
            boxed[to] = y_box(
                k % 4,
                plane_z[pl.ds(k * ny, ny), pl.ds(nz, nz)],
                [row_of(t, count + k, 1) for t in (2, 3)],
                [row_of(t, count + k, 1) for t in (4, 5)],
            )

    @pl.when(i < steps - 1)
    def _():
        edges = jnp.concatenate(
            [z_ref[pl.ds(i * blocks + b, 8, stride=zrows), :] for b in range(blocks)], axis=1
        )
        grid_z[...] = along_z(v_ref[...], edges, w_ref, e_ref)
        running = run[...]
        here = pl.ds(pl.multiple_of(i * PLANES, PLANES), PLANES)
        starts = rows_y[0, here, pl.ds(0, nz)]
        sides = {t: rows_y[t, here, pl.ds(nz, nz)] for t in (2, 3, 4, 5)}
        for p in range(PLANES):
            x = i * PLANES + p
            at = pl.ds(p * ny, ny)
            running = running + y_prefix(grid_z[at, pl.ds(0, nz)], starts[p : p + 1])
            prefix_ref[at, :] = running * F32(scale)
            boxed[x + 2] = y_box(
                p % 4,
                grid_z[at, pl.ds(nz, nz)],
                [sides[t][p : p + 1] for t in (2, 3)],
                [sides[t][p : p + 1] for t in (4, 5)],
            )
        run[...] = running

    @pl.when(i > 0)
    def _():
        for p in range(PLANES):
            x = (i - 1) * PLANES + p
            total = boxed[x]
            for d in range(1, 5):
                total = total + boxed[x + d]
            box_ref[pl.ds(p * ny, ny), :] = total * F32(1.0 / math.sqrt(125.0))


def fixed(*shape):
    return pl.BlockSpec(shape, lambda i: (0,) * len(shape))


def per_device(volume):
    cx, cy, cz = volume.shape
    nx, ny, nz = (lax.axis_size(a) for a in ("gx", "gy", "gz"))
    steps = cx // PLANES
    rows = PLANES * cy
    zrows = cx * cy // 128
    flat = volume.reshape(cx * cy, cz)

    def of(*shape):
        return jax.ShapeDtypeStruct(shape, F32)

    faces = [(8, cy, cz), (8, cx + 8, cz), (8 * zrows, 128), (8, 8, cx), (4, 8, 2 * cy), (1, 8, 128)]
    x, y, z, zy, zx, zxy = pl.pallas_call(
        functools.partial(sources_kernel, cy, cz),
        grid=(steps,),
        in_specs=[pl.BlockSpec((rows, cz), lambda i: (i, 0))],
        out_specs=[fixed(*s) for s in faces],
        out_shape=[of(*s) for s in faces],
    )(flat)

    z = z.reshape(8, zrows, 128)
    vmem = pl.BlockSpec(memory_space=pltpu.VMEM)
    sent_shapes = [a.shape for a in (x, y, z, zy, zx, zxy)]
    copies = 4 * (nx + ny + nz) + 4
    lx, ly, lz = (max(n - 1, 1) for n in (nx, ny, nz))
    buffers = [
        (lx, cy, cz), (4, cy, cz),
        (ly, cx + 8, cz), (4, cx + 8, cz),
        (lz, zrows, 128), (4, zrows, 128),
        (ly, 8, cx), (4, 8, cx), (8, 8, cx),
        (lx, 8, 128), (2, 8, 128),
        (ny, 1, 8, 128),
        (9, 8, 128), (nx, 9, 8, 128),
        (8, 8, 128), (nz, 8, 8, 128),
        (5, 8, 128), (nz, 5, 8, 128),
    ]
    x, y, z, zy, zx, zxy = pl.pallas_call(
        exchange_kernel,
        in_specs=[vmem] * 6,
        out_specs=[vmem] * 6,
        out_shape=[of(*s) for s in sent_shapes],
        scratch_shapes=[pltpu.VMEM(s, F32) for s in buffers]
        + [pltpu.SemaphoreType.DMA((copies,)), pltpu.SemaphoreType.DMA((copies,))],
        compiler_params=pltpu.CompilerParams(collective_id=0, has_side_effects=True),
    )(x, y, z, zy, zx, zxy)
    z = z.reshape(8 * zrows, 128)

    weights, edge_weights = z_weights(cz)
    scale = 1.0 / math.sqrt(cx * nx * cy * ny * cz * nz)
    prefix, box = pl.pallas_call(
        functools.partial(final_kernel, cy, cz, scale),
        grid=(steps + 1,),
        in_specs=[pl.BlockSpec((rows, cz), lambda i: (jnp.minimum(i, steps - 1), 0))]
        + [fixed(*a.shape) for a in (x, y, z, zy, zx, zxy, weights, edge_weights)],
        out_specs=[
            pl.BlockSpec((rows, cz), lambda i: (jnp.minimum(i, steps - 1), 0)),
            pl.BlockSpec((rows, cz), lambda i: (jnp.maximum(i - 1, 0), 0)),
        ],
        out_shape=[of(cx * cy, cz), of(cx * cy, cz)],
        scratch_shapes=[
            pltpu.VMEM((rows, 2 * cz), F32),
            pltpu.VMEM((8, cx + 8, 2 * cz), F32),
            pltpu.VMEM((8 * cy, 2 * cz), F32),
            pltpu.VMEM((cy, cz), F32),
            pltpu.VMEM((4, cy + 16, cz), F32),
            pltpu.VMEM((cx + 4, cy, cz), F32),
        ],
        compiler_params=pltpu.CompilerParams(vmem_limit_bytes=48 * 1024 * 1024),
    )(flat, x, y, z, zy, zx, zxy, weights, edge_weights)
    return prefix.reshape(cx, cy, cz), box.reshape(cx, cy, cz)


def solution(mesh):
    return jax.shard_map(
        per_device,
        mesh=mesh,
        in_specs=(P("gx", "gy", "gz"),),
        out_specs=(P("gx", "gy", "gz"), P("gx", "gy", "gz")),
        check_vma=False,
    )
```

profile of v0, /device:TPU:0, one launch (start us, length us, event | category | flops | bytes accessed | tf_op | source)
XLA Modules:
  0.0 41.7 jit_solution(9997459587912425063)
XLA Ops:
  0.7 0.1 select_convert_fusion.2
  0.8 0.1 iota.47
  0.9 7.4 %shard_map.30 = (f32[8,64,128]{2,1,0:T(8,128)}, f32[8,136,128]{2,1,0:T(8,128)}, f32[512,128]{1,0:T(8,128)}, f32[8,8,128]{2,1,0:T(8,128)}, f32[4,8,128]{2,1,0:T(8,128)}, /*index=5*/f32[1,8,128]{2,1,0:T(8,128)}) custom-call(f32[8192,128]{1,0:T(8,128)} %bitcast.5), custom_call_target="tpu_custom_call" | custom-call | tf_op jit(solution)/shard_map/pallas_call | solution.py:359
  8.3 17.9 %shard_map.31 = (f32[8,64,128]{2,1,0:T(8,128)}, f32[8,136,128]{2,1,0:T(8,128)}, f32[8,64,128]{2,1,0:T(8,128)}, f32[8,8,128]{2,1,0:T(8,128)}, f32[4,8,128]{2,1,0:T(8,128)}, /*index=5*/f32[1,8,128]{2,1,0:T(8,128)}) custom-call(f32[8,64,128]{2,1,0:T(8,128)} %get-tuple-element.16.x_in, f32[8,136,128]{2,1,0:T(8,128)} %get-tuple-element.17.y_in, ...), custom_call_target="tpu_custom_call" | custom-call | tf_op jit(solution)/shard_map/pallas_call | solution.py:383
  26.2 0.0 copy-start
  26.2 2.2 %copy-done = f32[128,64,128]{2,1,0:T(8,128)S(1)} copy-done((f32[128,64,128]{2,1,0:T(8,128)S(1)}, f32[128,64,128]{2,1,0:T(8,128)}, u32[]{:S(2)}) %copy-start) | copy-done | bytes 4194328
  28.4 0.0 copy-start.1
  28.4 1.1 %copy-done.1 = f32[8,136,128]{2,1,0:T(8,128)S(1)} copy-done((f32[8,136,128]{2,1,0:T(8,128)S(1)}, f32[8,136,128]{2,1,0:T(8,128)}, u32[]{:S(2)}) %copy-start.1) | copy-done | bytes 557080
  29.4 0.0 copy-start.2
  29.4 0.9 %copy-done.2 = f32[8,64,128]{2,1,0:T(8,128)S(1)} copy-done((f32[8,64,128]{2,1,0:T(8,128)S(1)}, f32[8,64,128]{2,1,0:T(8,128)}, u32[]{:S(2)}) %copy-start.2) | copy-done | bytes 262168
  30.4 0.0 copy-start.3
  30.4 0.9 %copy-done.3 = f32[8,64,128]{2,1,0:T(8,128)S(1)} copy-done((f32[8,64,128]{2,1,0:T(8,128)S(1)}, f32[8,64,128]{2,1,0:T(8,128)}, u32[]{:S(2)}) %copy-start.3) | copy-done | bytes 262168
  31.3 0.0 copy-start.4
  31.3 0.8 %copy-done.4 = f32[8,8,128]{2,1,0:T(8,128)S(1)} copy-done((f32[8,8,128]{2,1,0:T(8,128)S(1)}, f32[8,8,128]{2,1,0:T(8,128)}, u32[]{:S(2)}) %copy-start.4) | copy-done | bytes 32792
  32.1 0.0 copy-start.5
  32.1 0.7 %copy-done.5 = f32[4,8,128]{2,1,0:T(8,128)S(1)} copy-done((f32[4,8,128]{2,1,0:T(8,128)S(1)}, f32[4,8,128]{2,1,0:T(8,128)}, u32[]{:S(2)}) %copy-start.5) | copy-done | bytes 16408
  32.8 0.0 copy-start.6
  32.8 0.7 %copy-done.6 = f32[1,8,128]{2,1,0:T(8,128)S(1)} copy-done((f32[1,8,128]{2,1,0:T(8,128)S(1)}, f32[1,8,128]{2,1,0:T(8,128)}, u32[]{:S(2)}) %copy-start.6) | copy-done | bytes 4120
  33.5 8.3 %shard_map.32 = (f32[8192,128]{1,0:T(8,128)}, f32[8192,128]{1,0:T(8,128)}) custom-call(f32[8192,128]{1,0:T(8,128)S(1)} %bitcast.6, f32[8,64,128]{2,1,0:T(8,128)S(1)} %copy-done.2, f32[8,136,128]{2,1,0:T(8,128)S(1)} %copy-done.1, f32[512,128]{1,0:T(8,128)S(1)} %bitcast.7, f32[8,8,128]{2,1,0:T(8,128)S(1)} %copy-done.4, f32[4,8,128]{2,1,0:T(8,128)S(1)} %copy-done.5, ...), custom_call_target="tpu_custom_call" | custom-call | tf_op jit(solution)/shard_map/pallas_call | solution.py:396
  (8 shorter events, 0.1 us)
Async XLA Ops:
  26.2 2.2 %copy-start = (f32[128,64,128]{2,1,0:T(8,128)S(1)}, f32[128,64,128]{2,1,0:T(8,128)}, u32[]{:S(2)}) copy-start(f32[128,64,128]{2,1,0:T(8,128)} %param.1) | copy-start | bytes 12582916
  28.4 1.1 %copy-start.1 = (f32[8,136,128]{2,1,0:T(8,128)S(1)}, f32[8,136,128]{2,1,0:T(8,128)}, u32[]{:S(2)}) copy-start(f32[8,136,128]{2,1,0:T(8,128)} %get-tuple-element.23.y_ref) | copy-start | bytes 1671172
  29.4 0.9 %copy-start.2 = (f32[8,64,128]{2,1,0:T(8,128)S(1)}, f32[8,64,128]{2,1,0:T(8,128)}, u32[]{:S(2)}) copy-start(f32[8,64,128]{2,1,0:T(8,128)} %get-tuple-element.22.x_ref) | copy-start | bytes 786436
  30.4 0.9 %copy-start.3 = (f32[8,64,128]{2,1,0:T(8,128)S(1)}, f32[8,64,128]{2,1,0:T(8,128)}, u32[]{:S(2)}) copy-start(f32[8,64,128]{2,1,0:T(8,128)} %get-tuple-element.24) | copy-start | bytes 786436
  31.3 0.8 %copy-start.4 = (f32[8,8,128]{2,1,0:T(8,128)S(1)}, f32[8,8,128]{2,1,0:T(8,128)}, u32[]{:S(2)}) copy-start(f32[8,8,128]{2,1,0:T(8,128)} %get-tuple-element.25.zy_ref) | copy-start | bytes 98308
  32.1 0.7 %copy-start.5 = (f32[4,8,128]{2,1,0:T(8,128)S(1)}, f32[4,8,128]{2,1,0:T(8,128)}, u32[]{:S(2)}) copy-start(f32[4,8,128]{2,1,0:T(8,128)} %get-tuple-element.26.zx_ref) | copy-start | bytes 49156
  32.8 0.7 %copy-start.6 = (f32[1,8,128]{2,1,0:T(8,128)S(1)}, f32[1,8,128]{2,1,0:T(8,128)}, u32[]{:S(2)}) copy-start(f32[1,8,128]{2,1,0:T(8,128)} %get-tuple-element.27.zxy_ref) | copy-start | bytes 12292
where the time goes:
time: 42.3 us; the launch traced here: 41.7 us
  Pallas kernels  33.5 us (79%)
  local copies, waits for them, and re-layouts  7.36 us (17%)
  between operations  0.7 us (2%)
    pallas_call x1, Pallas kernels, per_device(): pl.pallas_call(exchange_kernel, in_specs=[vmem] * 6, out_specs=[vmem] * 6...  17.9 us
    pallas_call x1, Pallas kernels, per_device(): pl.pallas_call(functools.partial(final_kernel, cy, cz, scale), grid=(step...  8.26 us
    pallas_call x1, Pallas kernels, per_device(): pl.pallas_call(functools.partial(sources_kernel, cy, cz), grid=(steps,),...  7.38 us
    unnamed x14, local copies, waits for them, and re-layouts  7.29 us

commit v1 on v0

v1 whole, which is shorter than its diff:
```python
import functools
import math

import jax
import jax.numpy as jnp
from jax import lax
from jax.experimental import pallas as pl
from jax.experimental.pallas import tpu as pltpu
from jax.sharding import PartitionSpec as P

F32 = jnp.float32
BF16 = jnp.bfloat16
MESH = pl.DeviceIdType.MESH
USED = (0, 2, 3, 4, 5)
PLANES = 32
CHUNKS = 4


def split(a, axis):
    hi = a.astype(BF16)
    lo = (a - hi.astype(F32)).astype(BF16)
    return jnp.concatenate([hi, lo], axis=axis)


def source_index(kind, length):
    return {2: length - 2, 3: length - 1, 4: 0, 5: 1}[kind]


def selector(length):
    kind = lax.broadcasted_iota(jnp.int32, (8, length), 0)
    at = lax.broadcasted_iota(jnp.int32, (8, length), 1)
    pick = kind == 0
    for k in (2, 3, 4, 5):
        pick = pick | ((kind == k) & (at == source_index(k, length)))
    one = jnp.where(pick, 1.0, 0.0).astype(BF16)
    return jnp.concatenate([one, one], axis=1)


def z_sources(rows):
    return lax.dot_general(
        selector(rows.shape[1]),
        split(rows, 1),
        (((1,), (1,)), ((), ())),
        preferred_element_type=F32,
    )


class Exchange:
    def __init__(self, send, recv):
        self.send, self.recv, self.count = send, recv, 0

    def start(self, axis, shift, src, dst):
        n, me = lax.axis_size(axis), lax.axis_index(axis)
        at = self.count
        self.count += 1
        copy = pltpu.make_async_remote_copy(
            src_ref=src,
            dst_ref=dst,
            send_sem=self.send.at[at],
            recv_sem=self.recv.at[at],
            device_id={axis: lax.rem(me + shift + n, n)},
            device_id_type=MESH,
        )
        sends = (me + shift >= 0) & (me + shift < n)
        receives = (me - shift >= 0) & (me - shift < n)
        pl.when(sends)(copy.start)
        return sends, receives, copy

    def layers(self, axis, src, carry, halo):
        out = []
        n = lax.axis_size(axis)
        if n > 1:
            out.append(self.start(axis, 1, src.at[pl.ds(2, 2)], halo.at[pl.ds(0, 2)]))
            out.append(self.start(axis, -1, src.at[pl.ds(4, 2)], halo.at[pl.ds(2, 2)]))
        for d in range(1, n):
            out.append(self.start(axis, d, src.at[pl.ds(0, 1)], carry.at[pl.ds(d - 1, 1)]))
        return out

    def whole(self, axis, src, slots):
        n = lax.axis_size(axis)
        out = [self.start(axis, d, src, slots.at[d - 1]) for d in range(1, n)]
        if n > 1:
            out.append(self.start(axis, -1, src, slots.at[n - 1]))
        return out


def arrived(copies):
    for _, receives, copy in copies:
        pl.when(receives)(copy.wait_recv)


def sent(copies):
    for sends, _, copy in copies:
        pl.when(sends)(copy.wait_send)


def carry_total(carry, n):
    total = carry[0]
    for d in range(1, n - 1):
        total = total + carry[d]
    return total


def put_layers(out_ref, carry, halo, n):
    out_ref[0] = carry_total(carry, n)
    out_ref[1] = jnp.zeros_like(out_ref[1])
    for k in range(4):
        out_ref[2 + k] = halo[k]
    for k in (6, 7):
        out_ref[k] = jnp.zeros_like(out_ref[k])


def combined(slots, n, kind):
    total = slots[0]
    for d in range(1, n - 1):
        total = total + slots[d]
    zero = jnp.zeros_like(total)
    result = jnp.where(kind == 0, total, zero)
    result = jnp.where((kind == 2) | (kind == 3), slots[0], result)
    return jnp.where((kind == 4) | (kind == 5), slots[n - 1], result)


def exchange_kernel(
    volume,
    v, x_out, y_out, xy_out, z_out, z1_out, z2_out,
    x_src, y_src, z_src, s_src, zx_src, corner, xx_src, corner_x, z1_src, z2_src,
    xc, xh, yc, yh, zc, zh, sc, sh, small, zxc, zxh, corner_y_in, xxc, xxh, corner_x_in,
    z1c, z1h, z2c, z2h, local, send, recv,
):
    sizes = {a: lax.axis_size(a) for a in ("gx", "gy", "gz")}
    nx, ny, nz = sizes["gx"], sizes["gy"], sizes["gz"]
    cx, cy, cz = v.shape
    part = cx // CHUNKS
    loads = []
    for c in range(CHUNKS):
        at = pl.ds(c * part, part)
        loads.append(pltpu.make_async_copy(volume.at[at], v.at[at], local.at[c]))
        loads[-1].start()
    for ref in (xc, xh, yc, yh, zc, zh, sc, sh, zxc, zxh, corner_y_in, xxc, xxh, corner_x_in,
                z1c, z1h, z2c, z2h):
        ref[...] = jnp.zeros_like(ref)
    barrier = pltpu.get_barrier_semaphore()
    for axis, n in sizes.items():
        me = lax.axis_index(axis)
        for d in range(1, n):
            pl.semaphore_signal(
                barrier, inc=1, device_id={axis: lax.rem(me + d, n)}, device_id_type=MESH
            )

    x_src[...] = jnp.zeros_like(x_src)
    s_src[...] = jnp.zeros_like(s_src)
    total = None
    for c in range(CHUNKS):
        at = pl.ds(c * part, part)
        loads[c].wait()
        planes = v[at]
        partial = jnp.sum(planes, axis=0)
        total = partial if total is None else total + partial
        y_src[0, at, :] = jnp.sum(planes, axis=1)
        for k in (2, 3, 4, 5):
            y_src[k, at, :] = planes[:, source_index(k, cy), :]
    x_src[0] = total
    for k in (2, 3, 4, 5):
        x_src[k] = v[source_index(k, cx)]
    pl.semaphore_wait(barrier, nx + ny + nz - 3)

    ex = Exchange(send, recv)
    to_y = ex.layers("gy", y_src, yc, yh)
    to_x = ex.layers("gx", x_src, xc, xh)
    blocks = part * cy // 128
    for c in range(CHUNKS):
        found = z_sources(v[pl.ds(c * part, part)].reshape(part * cy, cz))
        z_src[:, pl.ds(c * blocks, blocks), :] = found.reshape(8, blocks, 128)
    to_z = ex.layers("gz", z_src, zc, zh)

    planes = x_src[...]
    for k in USED:
        rows = jnp.sum(planes, axis=1) if k == 0 else planes[:, source_index(k, cy), :]
        s_src[k, pl.ds(0, 8), :] = rows
    zero = jnp.zeros((64, cz), F32)
    rows = [y_src[k] for k in USED] + [planes[:6].reshape(6 * cy, cz)]
    rows += [s_src[:, k, :] for k in range(8)] + [zero]
    found = z_sources(jnp.concatenate(rows, axis=0))
    for at, k in enumerate(USED):
        s_src[k, pl.ds(8, 8), :] = found[:, at * 128 : (at + 1) * 128]
    for k in range(3):
        zx_src[k] = found[:, (5 + k) * 128 : (6 + k) * 128]
    corner[0] = found[:, 8 * 128 : 9 * 128]
    to_y += ex.layers("gy", s_src, sc, sh)
    to_y += ex.whole("gy", corner, corner_y_in)
    to_x.append(ex.start("gx", 1, zx_src.at[pl.ds(1, 1)], zxh.at[pl.ds(0, 1)]))
    to_x.append(ex.start("gx", -1, zx_src.at[pl.ds(2, 1)], zxh.at[pl.ds(1, 1)]))
    for d in range(1, nx):
        to_x.append(ex.start("gx", d, zx_src.at[pl.ds(0, 1)], zxc.at[pl.ds(d - 1, 1)]))

    lane = lax.broadcasted_iota(jnp.int32, (1, 8, 128), 2)
    arrived(to_y)
    put_layers(small, sc, sh, ny)
    for k in range(8):
        xx_src[k] = small[:, k, :]
        z1_src[k] = small[:, 8 + k, :]
    corner_x[...] = combined(corner_y_in, ny, lax.rem(lane, 8))
    to_x += ex.layers("gx", xx_src, xxc, xxh)
    to_x += ex.whole("gx", corner_x, corner_x_in)
    to_z += ex.layers("gz", z1_src, z1c, z1h)
    put_layers(y_out, yc, yh, ny)

    arrived(to_x)
    pairs = [carry_total(zxc, nx), zxh[0], zxh[1], combined(corner_x_in, nx, lane // 8)[0]]
    for k in range(8):
        rows = [p[k : k + 1] for p in pairs] + [jnp.zeros((4, 128), F32)]
        z2_src[k] = jnp.concatenate(rows, axis=0)
    to_z += ex.layers("gz", z2_src, z2c, z2h)
    put_layers(x_out, xc, xh, nx)
    put_layers(xy_out, xxc, xxh, nx)

    arrived(to_z)
    put_layers(z_out, zc, zh, nz)
    put_layers(z1_out, z1c, z1h, nz)
    put_layers(z2_out, z2c, z2h, nz)
    sent(to_y + to_x + to_z)


def z_weights(nz):
    rows = lax.broadcasted_iota(jnp.int32, (nz, nz), 0)
    cols = lax.broadcasted_iota(jnp.int32, (nz, nz), 1)
    lower = jnp.where(rows <= cols, 1.0, 0.0).astype(BF16)
    band = jnp.where(jnp.abs(rows - cols) <= 2, 1.0, 0.0).astype(BF16)
    half = jnp.concatenate([lower, band], axis=1)
    kind = lax.broadcasted_iota(jnp.int32, (8, nz), 0)
    at = lax.broadcasted_iota(jnp.int32, (8, nz), 1)
    add = (kind == 2) & (at == 0)
    add |= (kind == 3) & (at <= 1)
    add |= (kind == 4) & (at >= nz - 2)
    add |= (kind == 5) & (at == nz - 1)
    edge = jnp.concatenate(
        [jnp.where(kind == 0, 1.0, 0.0).astype(BF16), jnp.where(add, 1.0, 0.0).astype(BF16)], axis=1
    )
    return jnp.concatenate([half, half], axis=0), jnp.concatenate([edge, edge], axis=0)


def along_z(rows, edges, w_ref, e_ref):
    main = jnp.dot(split(rows, 1), w_ref[...], preferred_element_type=F32)
    return main + lax.dot_general(
        split(edges, 0), e_ref[...], (((0,), (0,)), ((), ())), preferred_element_type=F32
    )


def final_kernel(
    ny, nz, scale,
    v_ref, x_ref, y_ref, xy_ref, z_ref, z1_ref, z2_ref, w_ref, e_ref,
    prefix_ref, box_ref,
    grid_z, rows_y, plane_z, corner_z, run, tall, boxed,
):
    i, steps = pl.program_id(0), pl.num_programs(0)
    count = y_ref.shape[1]
    blocks = PLANES * ny // 128
    zrows = z_ref.shape[0] // 8

    def y_prefix(piece, start):
        row = lax.broadcasted_iota(jnp.int32, (1, 8, nz), 1)
        c = piece.reshape(ny // 8, 8, nz)
        for step in (1, 2, 4):
            c = c + jnp.where(row >= step, pltpu.roll(c, step, 1), 0.0)
        out = []
        for k in range(ny // 8):
            out.append(c[k] + start)
            start = out[-1][7:8]
        return jnp.concatenate(out, axis=0)

    def y_box(slot, piece, before, after):
        tall[slot, pl.ds(8, ny), :] = piece
        tall[slot, pl.ds(6, 1), :] = before[0]
        tall[slot, pl.ds(7, 1), :] = before[1]
        tall[slot, pl.ds(8 + ny, 1), :] = after[0]
        tall[slot, pl.ds(9 + ny, 1), :] = after[1]
        total = piece
        for d in (6, 7, 9, 10):
            total = total + tall[slot, pl.ds(d, ny), :]
        return total

    def row_of(k, x, part):
        return corner_z[pl.ds(x * 8 + k, 1), pl.ds(part * nz, nz)]

    @pl.when(i == 0)
    def _():
        for k in USED:
            rows_y[k] = along_z(y_ref[k], z1_ref[:, k, :], w_ref, e_ref)
        corner_z[...] = along_z(xy_ref[...].reshape(64, nz), z2_ref[:, 3, :][:, :64], w_ref, e_ref)
        edges = jnp.concatenate([z2_ref[:, k, :] for k in range(3)], axis=1)
        plane_z[...] = along_z(x_ref[:6].reshape(6 * ny, nz), edges, w_ref, e_ref)
        run[...] = y_prefix(plane_z[pl.ds(0, ny), pl.ds(0, nz)], row_of(0, 0, 0))
        for k, to in ((2, 0), (3, 1), (4, count + 2), (5, count + 3)):
            boxed[to] = y_box(
                k % 4,
                plane_z[pl.ds(k * ny, ny), pl.ds(nz, nz)],
                [row_of(t, k, 1) for t in (2, 3)],
                [row_of(t, k, 1) for t in (4, 5)],
            )

    @pl.when(i < steps - 1)
    def _():
        edges = jnp.concatenate(
            [z_ref[pl.ds(i * blocks + b, 8, stride=zrows), :] for b in range(blocks)], axis=1
        )
        grid_z[...] = along_z(v_ref[pl.ds(i * PLANES * ny, PLANES * ny), :], edges, w_ref, e_ref)
        running = run[...]
        here = pl.ds(pl.multiple_of(i * PLANES, PLANES), PLANES)
        starts = rows_y[0, here, pl.ds(0, nz)]
        sides = {t: rows_y[t, here, pl.ds(nz, nz)] for t in (2, 3, 4, 5)}
        for p in range(PLANES):
            x = i * PLANES + p
            at = pl.ds(p * ny, ny)
            running = running + y_prefix(grid_z[at, pl.ds(0, nz)], starts[p : p + 1])
            prefix_ref[at, :] = running * F32(scale)
            boxed[x + 2] = y_box(
                p % 4,
                grid_z[at, pl.ds(nz, nz)],
                [sides[t][p : p + 1] for t in (2, 3)],
                [sides[t][p : p + 1] for t in (4, 5)],
            )
        run[...] = running

    @pl.when(i > 0)
    def _():
        for p in range(PLANES):
            x = (i - 1) * PLANES + p
            total = boxed[x]
            for d in range(1, 5):
                total = total + boxed[x + d]
            box_ref[pl.ds(p * ny, ny), :] = total * F32(1.0 / math.sqrt(125.0))


def per_device(volume):
    cx, cy, cz = volume.shape
    nx, ny, nz = (lax.axis_size(a) for a in ("gx", "gy", "gz"))
    steps = cx // PLANES
    rows = PLANES * cy
    zrows = cx * cy // 128

    def of(*shape):
        return jax.ShapeDtypeStruct(shape, F32)

    vmem = pl.BlockSpec(memory_space=pltpu.VMEM)
    copies = 8 * (nx + ny + nz) + 4
    lx, ly, lz = (max(n - 1, 1) for n in (nx, ny, nz))
    row = (8, 128)
    faces = [(cx, cy, cz), (8, cy, cz), (8, cx, cz), (8, 8, cz), (8, zrows, 128), (8, 8, cx), (8, 8, 128)]
    buffers = [
        (8, cy, cz), (8, cx, cz), (8, zrows, 128), (8, 16, 128), (3, *row),
        (1, *row), (8, *row), (1, *row), (8, *row), (8, *row),
        (lx, cy, cz), (4, cy, cz), (ly, cx, cz), (4, cx, cz), (lz, zrows, 128), (4, zrows, 128),
        (ly, 16, 128), (4, 16, 128), (8, 16, 128), (lx, *row), (2, *row), (ny, 1, *row),
        (lx, *row), (4, *row), (nx, 1, *row),
        (lz, *row), (4, *row), (lz, *row), (4, *row),
    ]
    held, x, y, xy, z, z1, z2 = pl.pallas_call(
        exchange_kernel,
        in_specs=[pl.BlockSpec(memory_space=pltpu.HBM)],
        out_specs=[vmem] * 7,
        out_shape=[of(*s) for s in faces],
        scratch_shapes=[pltpu.VMEM(s, F32) for s in buffers]
        + [pltpu.SemaphoreType.DMA((CHUNKS,))]
        + [pltpu.SemaphoreType.DMA((copies,)), pltpu.SemaphoreType.DMA((copies,))],
        compiler_params=pltpu.CompilerParams(
            collective_id=0, has_side_effects=True, vmem_limit_bytes=46 * 1024 * 1024
        ),
    )(volume)
    z = z.reshape(8 * zrows, 128)

    weights, edge_weights = z_weights(cz)
    scale = 1.0 / math.sqrt(cx * nx * cy * ny * cz * nz)
    prefix, box = pl.pallas_call(
        functools.partial(final_kernel, cy, cz, scale),
        grid=(steps + 1,),
        in_specs=[vmem] * 9,
        out_specs=[
            pl.BlockSpec((rows, cz), lambda i: (jnp.minimum(i, steps - 1), 0)),
            pl.BlockSpec((rows, cz), lambda i: (jnp.maximum(i - 1, 0), 0)),
        ],
        out_shape=[of(cx * cy, cz), of(cx * cy, cz)],
        scratch_shapes=[
            pltpu.VMEM((rows, 2 * cz), F32),
            pltpu.VMEM((6, cx, 2 * cz), F32),
            pltpu.VMEM((6 * cy, 2 * cz), F32),
            pltpu.VMEM((64, 2 * cz), F32),
            pltpu.VMEM((cy, cz), F32),
            pltpu.VMEM((4, cy + 16, cz), F32),
            pltpu.VMEM((cx + 4, cy, cz), F32),
        ],
        compiler_params=pltpu.CompilerParams(vmem_limit_bytes=24 * 1024 * 1024),
    )(held.reshape(cx * cy, cz), x, y, xy, z, z1, z2, weights, edge_weights)
    return prefix.reshape(cx, cy, cz), box.reshape(cx, cy, cz)


def solution(mesh):
    return jax.shard_map(
        per_device,
        mesh=mesh,
        in_specs=(P("gx", "gy", "gz"),),
        out_specs=(P("gx", "gy", "gz"), P("gx", "gy", "gz")),
        check_vma=False,
    )
```

time: 42.3 us -> 24.1 us (0.57)
  Pallas kernels: 33.5 us -> 23 us
  local copies, waits for them, and re-layouts: 7.36 us -> 0.07 us
    pallas_call x2 -> x1, Pallas kernels: 25.3 us -> 15.3 us  [per_device(): pl.pallas_call(exchange_kernel, in_specs=[pl.BlockSpec(memory_space=pltpu...]
    unnamed x14 -> x0, local copies, waits for them, and re-layouts: 7.29 us -> none
    pallas_call x1, Pallas kernels: 8.26 us -> 7.74 us  [per_device(): pl.pallas_call(functools.partial(final_kernel, cy, cz, scale), grid=(step...]
where the time goes in v1:
time: 24.1 us; the launch traced here: 23.9 us
  Pallas kernels  23 us (95%)
  between operations  0.68 us (3%)
    pallas_call x1, Pallas kernels, per_device(): pl.pallas_call(exchange_kernel, in_specs=[pl.BlockSpec(memory_space=pltpu...  15.3 us
    pallas_call x1, Pallas kernels, per_device(): pl.pallas_call(functools.partial(final_kernel, cy, cz, scale), grid=(step...  7.74 us

profile of v1, /device:TPU:0, one launch (start us, length us, event | category | flops | bytes accessed | tf_op | source)
XLA Modules:
  0.0 23.9 jit_solution(15733203235843426228)
XLA Ops:
  0.7 0.1 select_convert_fusion.2
  0.8 0.1 iota.47
  0.9 15.3 %shard_map.30 = (f32[128,64,128]{2,1,0:T(8,128)S(1)}, f32[8,64,128]{2,1,0:T(8,128)S(1)}, f32[8,128,128]{2,1,0:T(8,128)S(1)}, f32[8,8,128]{2,1,0:T(8,128)S(1)}, f...) custom-call(f32[128,64,128]{2,1,0:T(8,128)} %volume.1), custom_call_target="tpu_custom_call" | custom-call | tf_op jit(solution)/shard_map/pallas_call | solution.py:357
  16.2 7.7 %shard_map.31 = (f32[8192,128]{1,0:T(8,128)}, f32[8192,128]{1,0:T(8,128)}) custom-call(f32[8192,128]{1,0:T(8,128)S(1)} %bitcast.4, f32[8,64,128]{2,1,0:T(8,128)S(1)} %get-tuple-element.12.x_ref, f32[8,128,128]{2,1,0:T(8,128)S(1)} %get-tuple-element.13.y_ref, f32[8,8,128]{2,1,0:T(8,128)S(1)} %get-tuple-element.14.xy_ref, f32[512,128]{1,0:T(8,128)S(1)} %bitcast.5, ...), custom_call_target="tpu_custom_call" | custom-call | tf_op jit(solution)/shard_map/pallas_call | solution.py:373
  (8 shorter events, 0.1 us)

commit v2 on v1

--- a/solution.py
+++ b/solution.py
@@ -121,9 +121,9 @@
 
 
 def exchange_kernel(
-    volume,
-    v, x_out, y_out, xy_out, z_out, z1_out, z2_out,
-    x_src, y_src, z_src, s_src, zx_src, corner, xx_src, corner_x, z1_src, z2_src,
+    volume, w_ref,
+    sum_out, box_out, x_out, y_out, xy_out, z_out, z1_out, z2_out,
+    v, grid_z, tall, x_src, y_src, z_src, s_src, zx_src, corner, xx_src, corner_x, z1_src, z2_src,
     xc, xh, yc, yh, zc, zh, sc, sh, small, zxc, zxh, corner_y_in, xxc, xxh, corner_x_in,
     z1c, z1h, z2c, z2h, local, send, recv,
 ):
@@ -147,6 +147,8 @@
                 barrier, inc=1, device_id={axis: lax.rem(me + d, n)}, device_id_type=MESH
             )
 
+    tall[:, pl.ds(0, 8), :] = jnp.zeros((part, 8, cz), F32)
+    tall[:, pl.ds(8 + cy, 8), :] = jnp.zeros((part, 8, cz), F32)
     x_src[...] = jnp.zeros_like(x_src)
     s_src[...] = jnp.zeros_like(s_src)
     total = None
@@ -193,6 +195,28 @@
     for d in range(1, nx):
         to_x.append(ex.start("gx", d, zx_src.at[pl.ds(0, 1)], zxc.at[pl.ds(d - 1, 1)]))
 
+    def own_sums(c):
+        at = pl.ds(c * part, part)
+        rows = split(v[at].reshape(part * cy, cz), 1)
+        grid_z[...] = jnp.dot(rows, w_ref[...], preferred_element_type=F32)
+        row = lax.broadcasted_iota(jnp.int32, (1, 8, cz), 1)
+        tiles = grid_z[:, pl.ds(0, cz)].reshape(part * cy // 8, 8, cz)
+        for step in (1, 2, 4):
+            tiles = tiles + jnp.where(row >= step, pltpu.roll(tiles, step, 1), 0.0)
+        tiles = tiles.reshape(part, cy // 8, 8, cz)
+        start = None
+        for k in range(cy // 8):
+            now = tiles[:, k] if k == 0 else tiles[:, k] + start
+            sum_out[at, pl.ds(8 * k, 8), :] = now
+            start = now[:, 7:8, :]
+        main = grid_z[:, pl.ds(cz, cz)].reshape(part, cy, cz)
+        tall[:, pl.ds(8, cy), :] = main
+        for d in (6, 7, 9, 10):
+            main = main + tall[:, pl.ds(d, cy), :]
+        box_out[at] = main
+
+    for c in range(CHUNKS // 2):
+        own_sums(c)
     lane = lax.broadcasted_iota(jnp.int32, (1, 8, 128), 2)
     arrived(to_y)
     put_layers(small, sc, sh, ny)
@@ -204,6 +228,8 @@
     to_x += ex.whole("gx", corner_x, corner_x_in)
     to_z += ex.layers("gz", z1_src, z1c, z1h)
     put_layers(y_out, yc, yh, ny)
+    for c in range(CHUNKS // 2, CHUNKS):
+        own_sums(c)
 
     arrived(to_x)
     pairs = [carry_total(zxc, nx), zxh[0], zxh[1], combined(corner_x_in, nx, lane // 8)[0]]
@@ -239,6 +265,16 @@
     return jnp.concatenate([half, half], axis=0), jnp.concatenate([edge, edge], axis=0)
 
 
+def y_weights(ny):
+    rows = lax.broadcasted_iota(jnp.int32, (128, 128), 0)
+    cols = lax.broadcasted_iota(jnp.int32, (128, 128), 1)
+    same = rows // ny == cols // ny
+    lower = jnp.where(same & (rows <= cols), 1.0, 0.0).astype(BF16)
+    band = jnp.where(same & (jnp.abs(rows - cols) <= 2), 1.0, 0.0).astype(BF16)
+    half = jnp.concatenate([lower, band], axis=1)
+    return jnp.concatenate([half, half], axis=0)
+
+
 def along_z(rows, edges, w_ref, e_ref):
     main = jnp.dot(split(rows, 1), w_ref[...], preferred_element_type=F32)
     return main + lax.dot_general(
@@ -248,9 +284,9 @@
 
 def final_kernel(
     ny, nz, scale,
-    v_ref, x_ref, y_ref, xy_ref, z_ref, z1_ref, z2_ref, w_ref, e_ref,
+    sum_ref, own_ref, x_ref, y_ref, xy_ref, z_ref, z1_ref, z2_ref, w_ref, e_ref, yw_ref,
     prefix_ref, box_ref,
-    grid_z, rows_y, plane_z, corner_z, run, tall, boxed,
+    edge_z, edge_y, rows_y, plane_z, corner_z, run, tall, boxed,
 ):
     i, steps = pl.program_id(0), pl.num_programs(0)
     count = y_ref.shape[1]
@@ -284,6 +320,9 @@
 
     @pl.when(i == 0)
     def _():
+        found = jnp.dot(split(z_ref[...], 1), yw_ref[...], preferred_element_type=F32)
+        edge_y[pl.ds(0, zrows), :] = found[:zrows, :128]
+        edge_y[pl.ds(zrows, 7 * zrows), :] = found[zrows:, 128:]
         for k in USED:
             rows_y[k] = along_z(y_ref[k], z1_ref[:, k, :], w_ref, e_ref)
         corner_z[...] = along_z(xy_ref[...].reshape(64, nz), z2_ref[:, 3, :][:, :64], w_ref, e_ref)
@@ -301,24 +340,28 @@
     @pl.when(i < steps - 1)
     def _():
         edges = jnp.concatenate(
-            [z_ref[pl.ds(i * blocks + b, 8, stride=zrows), :] for b in range(blocks)], axis=1
+            [edge_y[pl.ds(i * blocks + b, 8, stride=zrows), :] for b in range(blocks)], axis=1
         )
-        grid_z[...] = along_z(v_ref[pl.ds(i * PLANES * ny, PLANES * ny), :], edges, w_ref, e_ref)
+        edge_z[...] = lax.dot_general(
+            split(edges, 0), e_ref[...], (((0,), (0,)), ((), ())), preferred_element_type=F32
+        )
         running = run[...]
         here = pl.ds(pl.multiple_of(i * PLANES, PLANES), PLANES)
         starts = rows_y[0, here, pl.ds(0, nz)]
-        sides = {t: rows_y[t, here, pl.ds(nz, nz)] for t in (2, 3, 4, 5)}
+        b2, b1, a1, a2 = (rows_y[t, here, pl.ds(nz, nz)] for t in (2, 3, 4, 5))
+        below, above = b2 + b1, a1 + a2
+        row = lax.broadcasted_iota(jnp.int32, (8, nz), 0)
         for p in range(PLANES):
             x = i * PLANES + p
             at = pl.ds(p * ny, ny)
-            running = running + y_prefix(grid_z[at, pl.ds(0, nz)], starts[p : p + 1])
+            running = running + (sum_ref[x] + edge_z[at, pl.ds(0, nz)] + starts[p : p + 1])
             prefix_ref[at, :] = running * F32(scale)
-            boxed[x + 2] = y_box(
-                p % 4,
-                grid_z[at, pl.ds(nz, nz)],
-                [sides[t][p : p + 1] for t in (2, 3)],
-                [sides[t][p : p + 1] for t in (4, 5)],
-            )
+            own = own_ref[x] + edge_z[at, pl.ds(nz, nz)]
+            low = jnp.where(row == 0, below[p : p + 1], jnp.where(row == 1, b1[p : p + 1], 0.0))
+            top = jnp.where(row == 7, above[p : p + 1], jnp.where(row == 6, a1[p : p + 1], 0.0))
+            boxed[x + 2, pl.ds(0, 8), :] = own[:8] + low
+            boxed[x + 2, pl.ds(8, ny - 16), :] = own[8 : ny - 8]
+            boxed[x + 2, pl.ds(ny - 8, 8), :] = own[ny - 8 :] + top
         run[...] = running
 
     @pl.when(i > 0)
@@ -342,11 +385,13 @@
         return jax.ShapeDtypeStruct(shape, F32)
 
     vmem = pl.BlockSpec(memory_space=pltpu.VMEM)
+    weights, edge_weights = z_weights(cz)
     copies = 8 * (nx + ny + nz) + 4
     lx, ly, lz = (max(n - 1, 1) for n in (nx, ny, nz))
     row = (8, 128)
-    faces = [(cx, cy, cz), (8, cy, cz), (8, cx, cz), (8, 8, cz), (8, zrows, 128), (8, 8, cx), (8, 8, 128)]
+    faces = [(cx, cy, cz), (cx, cy, cz), (8, cy, cz), (8, cx, cz), (8, 8, cz), (8, zrows, 128), (8, 8, cx), (8, 8, 128)]
     buffers = [
+        (cx, cy, cz), (cx // CHUNKS * cy, 2 * cz), (cx // CHUNKS, cy + 16, cz),
         (8, cy, cz), (8, cx, cz), (8, zrows, 128), (8, 16, 128), (3, *row),
         (1, *row), (8, *row), (1, *row), (8, *row), (8, *row),
         (lx, cy, cz), (4, cy, cz), (ly, cx, cz), (4, cx, cz), (lz, zrows, 128), (4, zrows, 128),
@@ -354,26 +399,25 @@
         (lx, *row), (4, *row), (nx, 1, *row),
         (lz, *row), (4, *row), (lz, *row), (4, *row),
     ]
-    held, x, y, xy, z, z1, z2 = pl.pallas_call(
+    own_sum, own_box, x, y, xy, z, z1, z2 = pl.pallas_call(
         exchange_kernel,
-        in_specs=[pl.BlockSpec(memory_space=pltpu.HBM)],
-        out_specs=[vmem] * 7,
+        in_specs=[pl.BlockSpec(memory_space=pltpu.HBM), vmem],
+        out_specs=[vmem] * 8,
         out_shape=[of(*s) for s in faces],
         scratch_shapes=[pltpu.VMEM(s, F32) for s in buffers]
         + [pltpu.SemaphoreType.DMA((CHUNKS,))]
         + [pltpu.SemaphoreType.DMA((copies,)), pltpu.SemaphoreType.DMA((copies,))],
         compiler_params=pltpu.CompilerParams(
-            collective_id=0, has_side_effects=True, vmem_limit_bytes=46 * 1024 * 1024
+            collective_id=0, has_side_effects=True, vmem_limit_bytes=44 * 1024 * 1024
         ),
-    )(volume)
+    )(volume, weights)
     z = z.reshape(8 * zrows, 128)
 
-    weights, edge_weights = z_weights(cz)
     scale = 1.0 / math.sqrt(cx * nx * cy * ny * cz * nz)
     prefix, box = pl.pallas_call(
         functools.partial(final_kernel, cy, cz, scale),
         grid=(steps + 1,),
-        in_specs=[vmem] * 9,
+        in_specs=[vmem] * 11,
         out_specs=[
             pl.BlockSpec((rows, cz), lambda i: (jnp.minimum(i, steps - 1), 0)),
             pl.BlockSpec((rows, cz), lambda i: (jnp.maximum(i - 1, 0), 0)),
@@ -381,6 +425,7 @@
         out_shape=[of(cx * cy, cz), of(cx * cy, cz)],
         scratch_shapes=[
             pltpu.VMEM((rows, 2 * cz), F32),
+            pltpu.VMEM((8 * zrows, 128), F32),
             pltpu.VMEM((6, cx, 2 * cz), F32),
             pltpu.VMEM((6 * cy, 2 * cz), F32),
             pltpu.VMEM((64, 2 * cz), F32),
@@ -389,7 +434,7 @@
             pltpu.VMEM((cx + 4, cy, cz), F32),
         ],
         compiler_params=pltpu.CompilerParams(vmem_limit_bytes=24 * 1024 * 1024),
-    )(held.reshape(cx * cy, cz), x, y, xy, z, z1, z2, weights, edge_weights)
+    )(own_sum, own_box, x, y, xy, z, z1, z2, weights, edge_weights, y_weights(cy))
     return prefix.reshape(cx, cy, cz), box.reshape(cx, cy, cz)
 
 

time: 24.1 us -> 22.4 us (0.929)
  Pallas kernels: 23 us -> 21.1 us
    pallas_call x1, Pallas kernels: 7.74 us -> 5.68 us  [per_device(): pl.pallas_call(functools.partial(final_kernel, cy, cz, scale), grid=(step...]
where the time goes in v2:
time: 22.4 us; the launch traced here: 22.2 us
  Pallas kernels  21.1 us (94%)
  between operations  0.71 us (3%)
  other arithmetic  0.3 us (1%)
    pallas_call x1, Pallas kernels, per_device(): pl.pallas_call(exchange_kernel, in_specs=[pl.BlockSpec(memory_space=pltpu...  15.5 us
    pallas_call x1, Pallas kernels, per_device(): pl.pallas_call(functools.partial(final_kernel, cy, cz, scale), grid=(step...  5.68 us

profile of v2, /device:TPU:0, one launch (start us, length us, event | category | flops | bytes accessed | tf_op | source)
XLA Modules:
  0.0 22.2 jit_solution(7800685383157201758)
XLA Ops:
  0.7 0.1 select_convert_fusion.4
  0.8 0.1 iota.87
  0.9 0.1 select_convert_fusion.1
  1.1 15.5 %shard_map.30 = (f32[128,64,128]{2,1,0:T(8,128)S(1)}, f32[128,64,128]{2,1,0:T(8,128)S(1)}, f32[8,64,128]{2,1,0:T(8,128)S(1)}, f32[8,128,128]{2,1,0:T(8,128)S(1)}...) custom-call(f32[128,64,128]{2,1,0:T(8,128)} %volume.1, ...), custom_call_target="tpu_custom_call" | custom-call | tf_op jit(solution)/shard_map/pallas_call | solution.py:402
  16.5 5.7 %shard_map.31 = (f32[8192,128]{1,0:T(8,128)}, f32[8192,128]{1,0:T(8,128)}) custom-call(f32[128,64,128]{2,1,0:T(8,128)S(1)} %get-tuple-element.12.sum_ref, f32[128,64,128]{2,1,0:T(8,128)S(1)} %get-tuple-element.13.own_ref, f32[8,64,128]{2,1,0:T(8,128)S(1)} %get-tuple-element.14.x_ref, f32[8,128,128]{2,1,0:T(8,128)S(1)} %get-tuple-element.15.y_ref, ...), custom_call_target="tpu_custom_call" | custom-call | tf_op jit(solution)/shard_map/pallas_call | solution.py:417
  (11 shorter events, 0.1 us)

commit v3 on v2

--- a/solution.py
+++ b/solution.py
@@ -169,12 +169,6 @@
     ex = Exchange(send, recv)
     to_y = ex.layers("gy", y_src, yc, yh)
     to_x = ex.layers("gx", x_src, xc, xh)
-    blocks = part * cy // 128
-    for c in range(CHUNKS):
-        found = z_sources(v[pl.ds(c * part, part)].reshape(part * cy, cz))
-        z_src[:, pl.ds(c * blocks, blocks), :] = found.reshape(8, blocks, 128)
-    to_z = ex.layers("gz", z_src, zc, zh)
-
     planes = x_src[...]
     for k in USED:
         rows = jnp.sum(planes, axis=1) if k == 0 else planes[:, source_index(k, cy), :]
@@ -195,6 +189,12 @@
     for d in range(1, nx):
         to_x.append(ex.start("gx", d, zx_src.at[pl.ds(0, 1)], zxc.at[pl.ds(d - 1, 1)]))
 
+    blocks = part * cy // 128
+    for c in range(CHUNKS):
+        found = z_sources(v[pl.ds(c * part, part)].reshape(part * cy, cz))
+        z_src[:, pl.ds(c * blocks, blocks), :] = found.reshape(8, blocks, 128)
+    to_z = ex.layers("gz", z_src, zc, zh)
+
     def own_sums(c):
         at = pl.ds(c * part, part)
         rows = split(v[at].reshape(part * cy, cz), 1)
@@ -215,8 +215,6 @@
             main = main + tall[:, pl.ds(d, cy), :]
         box_out[at] = main
 
-    for c in range(CHUNKS // 2):
-        own_sums(c)
     lane = lax.broadcasted_iota(jnp.int32, (1, 8, 128), 2)
     arrived(to_y)
     put_layers(small, sc, sh, ny)
@@ -228,7 +226,7 @@
     to_x += ex.whole("gx", corner_x, corner_x_in)
     to_z += ex.layers("gz", z1_src, z1c, z1h)
     put_layers(y_out, yc, yh, ny)
-    for c in range(CHUNKS // 2, CHUNKS):
+    for c in range(CHUNKS // 2):
         own_sums(c)
 
     arrived(to_x)
@@ -240,6 +238,8 @@
     put_layers(x_out, xc, xh, nx)
     put_layers(xy_out, xxc, xxh, nx)
 
+    for c in range(CHUNKS // 2, CHUNKS):
+        own_sums(c)
     arrived(to_z)
     put_layers(z_out, zc, zh, nz)
     put_layers(z1_out, z1c, z1h, nz)

time: 22.4 us -> 22.2 us (level)
  no operation moved by 1% of the time
where the time goes in v3:
time: 22.2 us; the launch traced here: 22.1 us
  Pallas kernels  21 us (95%)
  between operations  0.71 us (3%)
  other arithmetic  0.3 us (1%)
    pallas_call x1, Pallas kernels, per_device(): pl.pallas_call(exchange_kernel, in_specs=[pl.BlockSpec(memory_space=pltpu...  15.3 us
    pallas_call x1, Pallas kernels, per_device(): pl.pallas_call(functools.partial(final_kernel, cy, cz, scale), grid=(step...  5.68 us

profile of v3, /device:TPU:0, one launch (start us, length us, event | category | flops | bytes accessed | tf_op | source)
XLA Modules:
  0.0 22.1 jit_solution(6573716842800030957)
XLA Ops:
  0.7 0.1 select_convert_fusion.4
  0.8 0.1 iota.87
  0.9 0.1 select_convert_fusion.1
  1.1 15.3 %shard_map.30 = (f32[128,64,128]{2,1,0:T(8,128)S(1)}, f32[128,64,128]{2,1,0:T(8,128)S(1)}, f32[8,64,128]{2,1,0:T(8,128)S(1)}, f32[8,128,128]{2,1,0:T(8,128)S(1)}...) custom-call(f32[128,64,128]{2,1,0:T(8,128)} %volume.1, ...), custom_call_target="tpu_custom_call" | custom-call | tf_op jit(solution)/shard_map/pallas_call | solution.py:402
  16.4 5.7 %shard_map.31 = (f32[8192,128]{1,0:T(8,128)}, f32[8192,128]{1,0:T(8,128)}) custom-call(f32[128,64,128]{2,1,0:T(8,128)S(1)} %get-tuple-element.12.sum_ref, f32[128,64,128]{2,1,0:T(8,128)S(1)} %get-tuple-element.13.own_ref, f32[8,64,128]{2,1,0:T(8,128)S(1)} %get-tuple-element.14.x_ref, f32[8,128,128]{2,1,0:T(8,128)S(1)} %get-tuple-element.15.y_ref, ...), custom_call_target="tpu_custom_call" | custom-call | tf_op jit(solution)/shard_map/pallas_call | solution.py:417
  (11 shorter events, 0.1 us)
